TPU v7x, 32 devices: a whole 2x2x4 slice. The times are simulated.
32 devices in a mesh: narrow: 4 (over z), wide: 8 (over y, x, core).
Axes of the slice: x: 2, y: 2, z: 4, core: 2. Of those that a mesh axis runs over, the one named last changes fastest.
Arguments:
- hidden_in: bfloat16 [8, 2048, 2048], P('narrow', 'wide'), may hold values from -6 to 6
- out_grad: bfloat16 [8, 2048, 2048], P('narrow', 'wide'), may hold values from -6 to 6
- doc_lengths: int32 [8, 8], P('narrow'), may hold values from 1 to 1024, 2048 in all within a row
- attn_gain: bfloat16 [2048], P('narrow'), may hold values from 0.5 to 1.5
- w_query: bfloat16 [2048, 2048], P('narrow', 'wide'), may hold values from -0.125 to 0.125
- w_key: bfloat16 [2048, 2048], P('narrow', 'wide'), may hold values from -0.125 to 0.125
- w_value: bfloat16 [2048, 2048], P('narrow', 'wide'), may hold values from -0.125 to 0.125
- w_out: bfloat16 [2048, 2048], P('wide', 'narrow'), may hold values from -1 to 1
- mlp_gain: bfloat16 [2048], P('narrow'), may hold values from 0.5 to 1.5
- w_gate: bfloat16 [2048, 8192], P('narrow', 'wide'), may hold values from -0.125 to 0.125
- w_up: bfloat16 [2048, 8192], P('narrow', 'wide'), may hold values from -0.125 to 0.125
- w_down: bfloat16 [8192, 2048], P('wide', 'narrow'), may hold values from -0.0625 to 0.0625
Outputs:
- hidden_out: bfloat16 [8, 2048, 2048], P('narrow', 'wide')
- in_grad: bfloat16 [8, 2048, 2048], P('narrow', 'wide')
- grad_attn_gain: float32 [2048], P(('narrow', 'wide'))
- grad_w_query: float32 [2048, 2048], P('narrow', 'wide')
- grad_w_key: float32 [2048, 2048], P('narrow', 'wide')
- grad_w_value: float32 [2048, 2048], P('narrow', 'wide')
- grad_w_out: float32 [2048, 2048], P('wide', 'narrow')
- grad_mlp_gain: float32 [2048], P(('narrow', 'wide'))
- grad_w_gate: float32 [2048, 8192], P('narrow', 'wide')
- grad_w_up: float32 [2048, 8192], P('narrow', 'wide')
- grad_w_down: float32 [8192, 2048], P('wide', 'narrow')
Inputs may be any that keep to these rules, and one draw needn't show every extreme that they name: `doc_lengths`: in every row the 8 lengths sum to 2048, and the longest is exactly 1024.
All inputs are finite; a program needn't handle non-finite values.
Results may differ from a plain program's by a relative error of at most 0.029.
Values may be sent and summed in bfloat16 or wider, within the bound.
No kernel may reach another device: no remote copies, remote signals or barrier semaphores. Data moves between devices by JAX's collectives and lax.ppermute only.
A program may use at most 192 MiB of HBM per device.

v0:
```python
import jax
import jax.numpy as jnp
from jax import lax
from jax.sharding import PartitionSpec as P

HEAD_DIM = 64
EPS = 1e-05
NEG = -1e30
ROPE_BASE = 130000.0


def mat_plain(left_op, right_op):
    return jnp.dot(left_op, right_op, preferred_element_type=jnp.float32)


def mat_back(left_op, right_op):
    return lax.dot_general(
        left_op, right_op, (((1,), (1,)), ((), ())), preferred_element_type=jnp.float32
    )


def mat_outer(left_op, right_op):
    return lax.dot_general(
        left_op, right_op, (((0,), (0,)), ((), ())), preferred_element_type=jnp.float32
    )


def rounded(values_in):
    return values_in.astype(jnp.bfloat16).astype(jnp.float32)


def doc_starts(lengths, seq_len):
    tokens = jnp.arange(seq_len, dtype=jnp.int32)
    ends_at = jnp.cumsum(lengths)
    before = jnp.where(ends_at[None, :] <= tokens[:, None], ends_at[None, :], jnp.int32(0))
    return jnp.max(before, axis=1)


def rope_tables(starts, seq_len):
    half_dim = HEAD_DIM // 2
    position = (jnp.arange(seq_len, dtype=jnp.int32) - starts).astype(jnp.float32)
    inverse = ROPE_BASE ** (-(jnp.arange(half_dim, dtype=jnp.float32) * 2.0) / HEAD_DIM)
    angles = position[:, None] * inverse[None, :]
    return (jnp.cos(angles)[:, None, :], jnp.sin(angles)[:, None, :])


def rotate(tensor, cos_table, sin_table):
    half_dim = tensor.shape[-1] // 2
    front_half = tensor[..., :half_dim]
    back_half = tensor[..., half_dim:]
    return jnp.concatenate(
        [
            front_half * cos_table - back_half * sin_table,
            back_half * cos_table + front_half * sin_table,
        ],
        axis=-1,
    )


def allowed_keys(starts, first_row, block_len, seq_len):
    row_ids = first_row + jnp.arange(block_len, dtype=jnp.int32)
    columns = jnp.arange(seq_len, dtype=jnp.int32)
    begins = lax.dynamic_slice_in_dim(starts, first_row, block_len)
    return (columns[None, :] <= row_ids[:, None]) & (columns[None, :] >= begins[:, None])


def attend_forward(queries, keys_rot, values_in, starts, block_len):
    seq_len, heads_here, head_size = queries.shape
    n_blocks = seq_len // block_len
    score_scale = head_size ** (-0.5)
    blocks = queries.reshape(n_blocks, block_len, heads_here, head_size)
    firsts = jnp.arange(n_blocks, dtype=jnp.int32) * block_len

    def one_block(block_pair):
        q_block, first_row = block_pair
        allowed = allowed_keys(starts, first_row, block_len, seq_len)
        scores = (
            jnp.einsum("qhd,khd->hqk", q_block, keys_rot, preferred_element_type=jnp.float32)
            * score_scale
        )
        masked = jnp.where(allowed[None], scores, NEG)
        row_max = jnp.max(masked, axis=-1, keepdims=True)
        exp_terms = jnp.exp(masked - row_max)
        row_total = jnp.sum(exp_terms, axis=-1, keepdims=True)
        prob_rows = (exp_terms / row_total).astype(jnp.bfloat16)
        block_out = jnp.einsum(
            "hqk,khd->qhd", prob_rows, values_in, preferred_element_type=jnp.float32
        )
        return (block_out, (row_max + jnp.log(row_total))[..., 0])

    block_outs, log_totals = lax.map(one_block, (blocks, firsts))
    return (block_outs.reshape(seq_len, heads_here * head_size), log_totals)


def attend_backward(queries, keys_rot, values_in, grad_att, log_totals, starts, block_len):
    seq_len, heads_here, head_size = queries.shape
    n_blocks = seq_len // block_len
    score_scale = head_size ** (-0.5)
    q_blocks = queries.reshape(n_blocks, block_len, heads_here, head_size)
    g_blocks = grad_att.reshape(n_blocks, block_len, heads_here, head_size)
    firsts = jnp.arange(n_blocks, dtype=jnp.int32) * block_len

    def one_block(carried, block_pack):
        key_acc, value_acc = carried
        q_block, g_block, lse_block, first_row = block_pack
        allowed = allowed_keys(starts, first_row, block_len, seq_len)
        scores = (
            jnp.einsum("qhd,khd->hqk", q_block, keys_rot, preferred_element_type=jnp.float32)
            * score_scale
        )
        masked = jnp.where(allowed[None], scores, NEG)
        probs_full = jnp.exp(masked - lse_block[..., None])
        prob_rows = probs_full.astype(jnp.bfloat16)
        value_acc = value_acc + jnp.einsum(
            "hqk,qhd->khd", prob_rows, g_block, preferred_element_type=jnp.float32
        )
        grad_probs = jnp.einsum(
            "qhd,khd->hqk", g_block, values_in, preferred_element_type=jnp.float32
        )
        row_inner = jnp.sum(probs_full * grad_probs, axis=-1, keepdims=True)
        grad_scores = (probs_full * (grad_probs - row_inner)).astype(jnp.bfloat16)
        query_grad = (
            jnp.einsum("hqk,khd->qhd", grad_scores, keys_rot, preferred_element_type=jnp.float32)
            * score_scale
        )
        key_acc = (
            key_acc
            + jnp.einsum("hqk,qhd->khd", grad_scores, q_block, preferred_element_type=jnp.float32)
            * score_scale
        )
        return ((key_acc, value_acc), query_grad)

    zero_field = jnp.zeros((seq_len, heads_here, head_size), jnp.float32)
    (key_grad, value_grad), query_grads = lax.scan(
        one_block, (zero_field, zero_field), (q_blocks, g_blocks, log_totals, firsts)
    )
    return (query_grads.reshape(seq_len, heads_here, head_size), key_grad, value_grad)


def one_row(input_row, grad_row, lengths, weights):
    inner_set, outer_set = weights
    w_query, w_key, w_value, w_gate, w_up, gain_attn, gain_mlp = inner_set
    w_out, w_down = outer_set
    attn_scale = gain_attn.astype(jnp.float32)
    mlp_scale = gain_mlp.astype(jnp.float32)
    local_rows = input_row.shape[0]
    seq_len = local_rows * lax.axis_size("wide")
    heads_here = w_query.shape[1] // HEAD_DIM
    block_len = min(512, seq_len)
    field_shape = (seq_len, heads_here, HEAD_DIM)
    flat_shape = (seq_len, heads_here * HEAD_DIM)
    starts = doc_starts(lengths, seq_len)
    cos_table, sin_table = rope_tables(starts, seq_len)
    residual = input_row.astype(jnp.float32)
    inv_first = lax.rsqrt(jnp.mean(residual * residual, axis=-1, keepdims=True) + EPS)
    normed = residual * inv_first
    attn_in = lax.all_gather((normed * attn_scale).astype(jnp.bfloat16), "wide", axis=0, tiled=True)
    queries = rotate(mat_plain(attn_in, w_query).reshape(field_shape), cos_table, sin_table).astype(
        jnp.bfloat16
    )
    keys_rot = rotate(mat_plain(attn_in, w_key).reshape(field_shape), cos_table, sin_table).astype(
        jnp.bfloat16
    )
    values_in = mat_plain(attn_in, w_value).astype(jnp.bfloat16).reshape(field_shape)
    attended, log_totals = attend_forward(queries, keys_rot, values_in, starts, block_len)
    attended = attended.astype(jnp.bfloat16)
    middle = residual + lax.psum_scatter(
        rounded(mat_plain(attended, w_out)).astype(jnp.bfloat16),
        "wide",
        scatter_dimension=0,
        tiled=True,
    ).astype(jnp.float32)
    inv_second = lax.rsqrt(jnp.mean(middle * middle, axis=-1, keepdims=True) + EPS)
    normed_mid = middle * inv_second
    mlp_in = lax.all_gather(
        (normed_mid * mlp_scale).astype(jnp.bfloat16), "wide", axis=0, tiled=True
    )
    gate_pre = mat_plain(mlp_in, w_gate)
    up_pre = mat_plain(mlp_in, w_up)
    sigmoid_gate = jax.nn.sigmoid(gate_pre)
    silu_gate = gate_pre * sigmoid_gate
    hidden = (silu_gate * up_pre).astype(jnp.bfloat16)
    output = middle + lax.psum_scatter(
        rounded(mat_plain(hidden, w_down)).astype(jnp.bfloat16),
        "wide",
        scatter_dimension=0,
        tiled=True,
    ).astype(jnp.float32)
    grad_full = lax.all_gather(grad_row, "wide", axis=0, tiled=True)
    grad_down = mat_outer(hidden, grad_full)
    grad_hidden = mat_back(grad_full, w_down)
    grad_gate_pre = (
        grad_hidden * up_pre * sigmoid_gate * (1.0 + gate_pre * (1.0 - sigmoid_gate))
    ).astype(jnp.bfloat16)
    grad_up_pre = (grad_hidden * silu_gate).astype(jnp.bfloat16)
    grad_gate = mat_outer(mlp_in, grad_gate_pre)
    grad_up = mat_outer(mlp_in, grad_up_pre)
    grad_mlp_in = lax.psum_scatter(
        rounded(mat_back(grad_gate_pre, w_gate) + mat_back(grad_up_pre, w_up)).astype(jnp.bfloat16),
        "wide",
        scatter_dimension=0,
        tiled=True,
    ).astype(jnp.float32)
    scaled_mid = grad_mlp_in * mlp_scale
    gain_mlp_grad = jnp.sum(grad_mlp_in * normed_mid, axis=0)
    grad_middle = grad_row.astype(jnp.float32) + inv_second * (
        scaled_mid - normed_mid * jnp.mean(scaled_mid * normed_mid, axis=-1, keepdims=True)
    )
    grad_branch = lax.all_gather(grad_middle.astype(jnp.bfloat16), "wide", axis=0, tiled=True)
    grad_out = mat_outer(attended, grad_branch)
    grad_att = mat_back(grad_branch, w_out).astype(jnp.bfloat16).reshape(field_shape)
    query_grad, key_grad, value_grad = attend_backward(
        queries, keys_rot, values_in, grad_att, log_totals, starts, block_len
    )
    query_raw = rotate(query_grad, cos_table, -sin_table).reshape(flat_shape).astype(jnp.bfloat16)
    key_raw = rotate(key_grad, cos_table, -sin_table).reshape(flat_shape).astype(jnp.bfloat16)
    value_raw = value_grad.reshape(flat_shape).astype(jnp.bfloat16)
    grad_query = mat_outer(attn_in, query_raw)
    grad_key = mat_outer(attn_in, key_raw)
    grad_value = mat_outer(attn_in, value_raw)
    grad_attn_in = lax.psum_scatter(
        rounded(
            mat_back(query_raw, w_query) + mat_back(key_raw, w_key) + mat_back(value_raw, w_value)
        ).astype(jnp.bfloat16),
        "wide",
        scatter_dimension=0,
        tiled=True,
    ).astype(jnp.float32)
    scaled_in = grad_attn_in * attn_scale
    gain_attn_grad = jnp.sum(grad_attn_in * normed, axis=0)
    grad_input = grad_middle + inv_first * (
        scaled_in - normed * jnp.mean(scaled_in * normed, axis=-1, keepdims=True)
    )
    return (
        output.astype(jnp.bfloat16),
        grad_input.astype(jnp.bfloat16),
        (grad_query, grad_key, grad_value, grad_gate, grad_up),
        (grad_out, grad_down),
        (gain_attn_grad, gain_mlp_grad),
    )


def per_device(
    hidden_in,
    out_grad,
    doc_lengths,
    attn_gain,
    w_query,
    w_key,
    w_value,
    w_out,
    mlp_gain,
    w_gate,
    w_up,
    w_down,
):
    narrow_count = lax.axis_size("narrow")

    def fetch_weights():
        inner_set = (
            lax.all_gather(w_query, "narrow", axis=0, tiled=True),
            lax.all_gather(w_key, "narrow", axis=0, tiled=True),
            lax.all_gather(w_value, "narrow", axis=0, tiled=True),
            lax.all_gather(w_gate, "narrow", axis=0, tiled=True),
            lax.all_gather(w_up, "narrow", axis=0, tiled=True),
            lax.all_gather(attn_gain, "narrow", axis=0, tiled=True),
            lax.all_gather(mlp_gain, "narrow", axis=0, tiled=True),
        )
        outer_set = (
            lax.all_gather(w_out, "narrow", axis=1, tiled=True),
            lax.all_gather(w_down, "narrow", axis=1, tiled=True),
        )
        return (inner_set, outer_set)

    def share_grads(grads_in, grads_out):
        summed_in = (
            lax.psum_scatter(
                grads_in[0].astype(jnp.bfloat16), "narrow", scatter_dimension=0, tiled=True
            ).astype(jnp.float32),
            lax.psum_scatter(
                grads_in[1].astype(jnp.bfloat16), "narrow", scatter_dimension=0, tiled=True
            ).astype(jnp.float32),
            lax.psum_scatter(
                grads_in[2].astype(jnp.bfloat16), "narrow", scatter_dimension=0, tiled=True
            ).astype(jnp.float32),
            lax.psum_scatter(
                grads_in[3].astype(jnp.bfloat16), "narrow", scatter_dimension=0, tiled=True
            ).astype(jnp.float32),
            lax.psum_scatter(
                grads_in[4].astype(jnp.bfloat16), "narrow", scatter_dimension=0, tiled=True
            ).astype(jnp.float32),
        )
        summed_out = (
            lax.psum_scatter(
                grads_out[0].astype(jnp.bfloat16), "narrow", scatter_dimension=1, tiled=True
            ).astype(jnp.float32),
            lax.psum_scatter(
                grads_out[1].astype(jnp.bfloat16), "narrow", scatter_dimension=1, tiled=True
            ).astype(jnp.float32),
        )
        return (summed_in, summed_out)

    acc_in = tuple(
        (jnp.zeros(weight.shape, jnp.float32) for weight in (w_query, w_key, w_value, w_gate, w_up))
    )
    acc_out = tuple((jnp.zeros(weight.shape, jnp.float32) for weight in (w_out, w_down)))
    gain_acc = (
        jnp.zeros((attn_gain.shape[0] * narrow_count,), jnp.float32),
        jnp.zeros((mlp_gain.shape[0] * narrow_count,), jnp.float32),
    )

    def micro_step(carried, inputs):
        sum_in, sum_out, sum_gain = carried
        input_row, grad_row, lengths = inputs
        weights = fetch_weights()
        output, grad_input, grads_in, grads_out, grads_gain = one_row(
            input_row, grad_row, lengths, weights
        )
        grads_in, grads_out = share_grads(grads_in, grads_out)
        sum_in = tuple((acc_item + new_item for acc_item, new_item in zip(sum_in, grads_in)))
        sum_out = tuple((acc_item + new_item for acc_item, new_item in zip(sum_out, grads_out)))
        sum_gain = tuple((acc_item + new_item for acc_item, new_item in zip(sum_gain, grads_gain)))
        return ((sum_in, sum_out, sum_gain), (output, grad_input))

    carried, (outputs, in_grads) = lax.scan(
        micro_step, (acc_in, acc_out, gain_acc), (hidden_in, out_grad, doc_lengths)
    )
    sum_in, sum_out, sum_gain = carried
    gain_grads = (
        lax.psum_scatter(sum_gain[0], ("narrow", "wide"), scatter_dimension=0, tiled=True),
        lax.psum_scatter(sum_gain[1], ("narrow", "wide"), scatter_dimension=0, tiled=True),
    )
    return (
        outputs,
        in_grads,
        gain_grads[0],
        sum_in[0],
        sum_in[1],
        sum_in[2],
        sum_out[0],
        gain_grads[1],
        sum_in[3],
        sum_in[4],
        sum_out[1],
    )


def solution(mesh):
    in_specs = (
        P("narrow", "wide", None),
        P("narrow", "wide", None),
        P("narrow", None),
        P("narrow"),
        P("narrow", "wide"),
        P("narrow", "wide"),
        P("narrow", "wide"),
        P("wide", "narrow"),
        P("narrow"),
        P("narrow", "wide"),
        P("narrow", "wide"),
        P("wide", "narrow"),
    )
    out_specs = (
        P("narrow", "wide", None),
        P("narrow", "wide", None),
        P(("narrow", "wide")),
        P("narrow", "wide"),
        P("narrow", "wide"),
        P("narrow", "wide"),
        P("wide", "narrow"),
        P(("narrow", "wide")),
        P("narrow", "wide"),
        P("narrow", "wide"),
        P("wide", "narrow"),
    )
    return jax.shard_map(
        per_device, mesh=mesh, in_specs=in_specs, out_specs=out_specs, check_vma=False
    )
```

profile of v0, /device:TPU:0, one launch (start us, length us, event | category | flops | bytes accessed | tf_op | source)
XLA Modules:
  0.0 2786.1 jit_solution(1502561951740328314)
XLA Ops:
  7.3 2731.1 %while.62 = (s32[]{:T(128)}, f32[512,256]{1,0:T(8,128)}, f32[512,256]{1,0:T(8,128)}, f32[512,256]{1,0:T(8,128)}, f32[512,1024]{1,0:T(8,128)}, /*index=5*/f32[512...) while((s32[]{:T(128)}, f32[512,256]{1,0:T(8,128)}, ...), condition=%wide.region_27.28_spmd.clone, body=%wide.region_0.27_spmd.clone.sunk | while | flops 107088232448 | bytes 1211792128 | solution.py:325
  40.8 55.8 %all-gather.24.cloned.1.call-done = bf16[2048,2048]{1,0:T(8,128)(2,1)} async-done(((bf16[256,2048]{1,0:T(8,128)(2,1)}), bf16[2048,2048]{1,0:T(8,128)(2,1)}) %all-gather.24.cloned.1.call-update) | async-done | bytes 8388624 | tf_op jit(solution)/shard_map/while/body/eval_jaxpr/all_gather | solution.py:157
  102.6 23.6 all-gather.26.cloned.1.call-done
  133.0 22.1 all-gather.30.cloned.1.call-done
  161.1 74.7 %while.63 = (s32[]{:T(128)}, bf16[4,512,4,64]{1,3,2,0:T(8,128)(2,1)}, f32[4,4,512]{2,1,0:T(4,128)}, s32[4]{0:T(128)S(1)}, s32[2048]{0:T(1024)}, /*index=5*/bf16[...) while((s32[]{:T(128)}, ...), condition=%wide.region_7.7_spmd, body=%wide.region_4.6_spmd.sunk | while | flops 1127217664 | bytes 65874156 | solution.py:91
  263.1 54.9 %reduce-scatter.12.cloned.1.call-done = bf16[256,2048]{1,0:T(8,128)(2,1)} async-done(((bf16[2048,2048]{1,0:T(8,128)(2,1)}), bf16[256,2048]{1,0:T(8,128)(2,1)}) %reduce-scatter.12.cloned.1.call-update) | async-done | bytes 1048592 | tf_op jit(solution)/shard_map/while/body/eval_jaxpr/reduce_scatter | solution.py:167
  323.1 77.4 %all-gather.38.cloned.1.call-done = bf16[1024,2048]{1,0:T(8,128)(2,1)} async-done(((bf16[1024,512]{1,0:T(8,128)(2,1)}), bf16[1024,2048]{1,0:T(8,128)(2,1)}) %all-gather.38.cloned.1.call-update) | async-done | bytes 4194320 | tf_op jit(solution)/shard_map/while/body/eval_jaxpr/all_gather | solution.py:271
  400.4 55.0 %all-gather.40.cloned.1.call-done = bf16[1,2048,2048]{2,1,0:T(8,128)(2,1)} async-done(((bf16[1,256,2048]{2,1,0:T(8,128)(2,1)}), bf16[1,2048,2048]{2,1,0:T(8,128)(2,1)}) %all-gather.40.cloned.1.call-update) | async-done | bytes 8388624 | tf_op jit(solution)/shard_map/while/body/eval_jaxpr/all_gather | solution.py:189
  455.4 14.7 fusion.256
  470.1 67.7 %all-gather.36.cloned.1.call-done = bf16[2048,1024]{1,0:T(8,128)(2,1)} async-done(((bf16[512,1024]{1,0:T(8,128)(2,1)}), bf16[2048,1024]{1,0:T(8,128)(2,1)}) %all-gather.36.cloned.1.call-update) | async-done | bytes 4194320 | tf_op jit(solution)/shard_map/while/body/eval_jaxpr/all_gather | solution.py:264
  537.9 54.8 %all-gather.34.cloned.1.call-done = bf16[2048,2048]{1,0:T(8,128)(2,1)} async-done(((bf16[256,2048]{1,0:T(8,128)(2,1)}), bf16[2048,2048]{1,0:T(8,128)(2,1)}) %all-gather.34.cloned.1.call-update) | async-done | bytes 8388624 | tf_op jit(solution)/shard_map/while/body/eval_jaxpr/all_gather | solution.py:175
  592.7 14.4 fusion.255
  607.1 68.1 %all-gather.42.cloned.1.call-done = bf16[2048,1024]{1,0:T(8,128)(2,1)} async-done(((bf16[512,1024]{1,0:T(8,128)(2,1)}), bf16[2048,1024]{1,0:T(8,128)(2,1)}) %all-gather.42.cloned.1.call-update) | async-done | bytes 4194320 | tf_op jit(solution)/shard_map/while/body/eval_jaxpr/all_gather | solution.py:265
  675.2 21.8 multiply_convert_fusion.9
  697.0 14.4 fusion.257
  711.4 16.4 add_convert_fusion.9
  727.9 69.9 %reduce-scatter.14.cloned.1.call-done = bf16[256,2048]{1,0:T(8,128)(2,1)} async-done(((bf16[2048,2048]{1,0:T(8,128)(2,1)}), bf16[256,2048]{1,0:T(8,128)(2,1)}) %reduce-scatter.14.cloned.1.call-update) | async-done | bytes 1048592 | tf_op jit(solution)/shard_map/while/body/eval_jaxpr/reduce_scatter | solution.py:198
  804.7 14.3 fusion.260
  833.2 14.7 convolution_convert_fusion.27
  875.4 249.1 %while.64 = (s32[]{:T(128)}, f32[2048,4,64]{0,2,1:T(8,128)}, f32[2048,4,64]{0,2,1:T(8,128)}, f32[4,512,4,64]{1,0,3,2:T(4,128)}, bf16[4,512,4,64]{1,3,2,0:T(8,128...) while((s32[]{:T(128)}, f32[2048,4,64]{0,2,1:T(8,128)}, ...), condition=%wide.region_14.14_spmd.clone, body=%wide.region_12.13_spmd.clone.sunk | while | flops 2753165824 | bytes 183044368 | solution.py:134
  1169.6 15.7 add_convert_fusion.10
  1185.6 14.1 convolution_convert_fusion.29
  1221.5 72.0 %reduce-scatter.30.cloned.1.call-done = bf16[256,2048]{1,0:T(8,128)(2,1)} async-done(((bf16[2048,2048]{1,0:T(8,128)(2,1)}), bf16[256,2048]{1,0:T(8,128)(2,1)}) %reduce-scatter.30.cloned.1.call-update) | async-done | bytes 1048592 | tf_op jit(solution)/shard_map/while/body/eval_jaxpr/reduce_scatter | solution.py:221
  1295.6 72.7 %reduce-scatter.32.cloned.1.call-done = bf16[256,2048]{1,0:T(8,128)(2,1)} async-done(((bf16[2048,2048]{1,0:T(8,128)(2,1)}), bf16[256,2048]{1,0:T(8,128)(2,1)}) %reduce-scatter.32.cloned.1.call-update) | async-done | bytes 1048592 | tf_op jit(solution)/shard_map/while/body/eval_jaxpr/reduce_scatter | solution.py:183
  1404.3 55.7 %all-gather.24.cloned.1.call-done = bf16[2048,2048]{1,0:T(8,128)(2,1)} async-done(((bf16[256,2048]{1,0:T(8,128)(2,1)}), bf16[2048,2048]{1,0:T(8,128)(2,1)}) %all-gather.24.cloned.1.call-update) | async-done | bytes 8388624 | tf_op jit(solution)/shard_map/while/body/eval_jaxpr/all_gather | solution.py:157
  1466.0 23.5 all-gather.26.cloned.1.call-done
  1496.3 22.1 all-gather.30.cloned.1.call-done
  1524.4 74.7 %while.63 = (s32[]{:T(128)}, bf16[4,512,4,64]{1,3,2,0:T(8,128)(2,1)}, f32[4,4,512]{2,1,0:T(4,128)}, s32[4]{0:T(128)S(1)}, s32[2048]{0:T(1024)}, /*index=5*/bf16[...) while((s32[]{:T(128)}, ...), condition=%wide.region_7.7_spmd, body=%wide.region_4.6_spmd.sunk | while | flops 1127217664 | bytes 65874156 | solution.py:91
  1626.5 54.8 %reduce-scatter.12.cloned.1.call-done = bf16[256,2048]{1,0:T(8,128)(2,1)} async-done(((bf16[2048,2048]{1,0:T(8,128)(2,1)}), bf16[256,2048]{1,0:T(8,128)(2,1)}) %reduce-scatter.12.cloned.1.call-update) | async-done | bytes 1048592 | tf_op jit(solution)/shard_map/while/body/eval_jaxpr/reduce_scatter | solution.py:167
  1686.2 77.5 %all-gather.38.cloned.1.call-done = bf16[1024,2048]{1,0:T(8,128)(2,1)} async-done(((bf16[1024,512]{1,0:T(8,128)(2,1)}), bf16[1024,2048]{1,0:T(8,128)(2,1)}) %all-gather.38.cloned.1.call-update) | async-done | bytes 4194320 | tf_op jit(solution)/shard_map/while/body/eval_jaxpr/all_gather | solution.py:271
  1763.7 54.8 %all-gather.40.cloned.1.call-done = bf16[1,2048,2048]{2,1,0:T(8,128)(2,1)} async-done(((bf16[1,256,2048]{2,1,0:T(8,128)(2,1)}), bf16[1,2048,2048]{2,1,0:T(8,128)(2,1)}) %all-gather.40.cloned.1.call-update) | async-done | bytes 8388624 | tf_op jit(solution)/shard_map/while/body/eval_jaxpr/all_gather | solution.py:189
  1818.6 14.7 fusion.256
  1833.3 67.7 %all-gather.36.cloned.1.call-done = bf16[2048,1024]{1,0:T(8,128)(2,1)} async-done(((bf16[512,1024]{1,0:T(8,128)(2,1)}), bf16[2048,1024]{1,0:T(8,128)(2,1)}) %all-gather.36.cloned.1.call-update) | async-done | bytes 4194320 | tf_op jit(solution)/shard_map/while/body/eval_jaxpr/all_gather | solution.py:264
  1901.0 55.0 %all-gather.34.cloned.1.call-done = bf16[2048,2048]{1,0:T(8,128)(2,1)} async-done(((bf16[256,2048]{1,0:T(8,128)(2,1)}), bf16[2048,2048]{1,0:T(8,128)(2,1)}) %all-gather.34.cloned.1.call-update) | async-done | bytes 8388624 | tf_op jit(solution)/shard_map/while/body/eval_jaxpr/all_gather | solution.py:175
  1956.0 14.4 fusion.255
  1970.4 67.9 %all-gather.42.cloned.1.call-done = bf16[2048,1024]{1,0:T(8,128)(2,1)} async-done(((bf16[512,1024]{1,0:T(8,128)(2,1)}), bf16[2048,1024]{1,0:T(8,128)(2,1)}) %all-gather.42.cloned.1.call-update) | async-done | bytes 4194320 | tf_op jit(solution)/shard_map/while/body/eval_jaxpr/all_gather | solution.py:265
  2038.3 21.8 multiply_convert_fusion.9
  2060.2 14.4 fusion.257
  2074.5 16.4 add_convert_fusion.9
  2091.0 69.9 %reduce-scatter.14.cloned.1.call-done = bf16[256,2048]{1,0:T(8,128)(2,1)} async-done(((bf16[2048,2048]{1,0:T(8,128)(2,1)}), bf16[256,2048]{1,0:T(8,128)(2,1)}) %reduce-scatter.14.cloned.1.call-update) | async-done | bytes 1048592 | tf_op jit(solution)/shard_map/while/body/eval_jaxpr/reduce_scatter | solution.py:198
  2167.9 14.3 fusion.260
  2196.3 14.7 convolution_convert_fusion.27
  2238.6 249.0 %while.64 = (s32[]{:T(128)}, f32[2048,4,64]{0,2,1:T(8,128)}, f32[2048,4,64]{0,2,1:T(8,128)}, f32[4,512,4,64]{1,0,3,2:T(4,128)}, bf16[4,512,4,64]{1,3,2,0:T(8,128...) while((s32[]{:T(128)}, f32[2048,4,64]{0,2,1:T(8,128)}, ...), condition=%wide.region_14.14_spmd.clone, body=%wide.region_12.13_spmd.clone.sunk | while | flops 2753165824 | bytes 183044368 | solution.py:134
  2532.7 15.7 add_convert_fusion.10
  2548.7 14.1 convolution_convert_fusion.29
  2585.0 71.8 %reduce-scatter.30.cloned.1.call-done = bf16[256,2048]{1,0:T(8,128)(2,1)} async-done(((bf16[2048,2048]{1,0:T(8,128)(2,1)}), bf16[256,2048]{1,0:T(8,128)(2,1)}) %reduce-scatter.30.cloned.1.call-update) | async-done | bytes 1048592 | tf_op jit(solution)/shard_map/while/body/eval_jaxpr/reduce_scatter | solution.py:221
  2658.8 72.7 %reduce-scatter.32.cloned.1.call-done = bf16[256,2048]{1,0:T(8,128)(2,1)} async-done(((bf16[2048,2048]{1,0:T(8,128)(2,1)}), bf16[256,2048]{1,0:T(8,128)(2,1)}) %reduce-scatter.32.cloned.1.call-update) | async-done | bytes 1048592 | tf_op jit(solution)/shard_map/while/body/eval_jaxpr/reduce_scatter | solution.py:183
  2738.4 39.7 %all-reduce.2 = (f32[2048]{0:T(1024)S(1)}, f32[2048]{0:T(1024)S(1)}) all-reduce(f32[2048]{0:T(1024)} %get-tuple-element.247, f32[2048]{0:T(1024)} %get-tuple-element.252), channel_id=14, replica_groups=mesh['narrow'=4,'wide'=8] {'narrow','wide'}, use_global_device_ids=true, to_apply=%region_28.29.clone | all-reduce | flops 4096 | bytes 32768
  (633 shorter events, 1026.2 us)
Async XLA Ops:
  7.8 33.1 %all-gather.28.cloned.1.call-start = ((), (), s32[]{:S(2)}) async-start(), calls=%async_computation.13 | async-start | bytes 1310720 | tf_op jit(solution)/shard_map/while/body/eval_jaxpr/all_gather | solution.py:261
  8.5 88.1 %all-gather.24.cloned.1.call-start = ((), (), s32[]{:S(2)}) async-start(), calls=%async_computation.11 | async-start | bytes 9437184 | tf_op jit(solution)/shard_map/while/body/eval_jaxpr/all_gather | solution.py:157
  27.4 98.7 %all-gather.26.cloned.1.call-start = ((), (), s32[]{:S(2)}) async-start(), calls=%async_computation.12 | async-start | bytes 1310720 | tf_op jit(solution)/shard_map/while/body/eval_jaxpr/all_gather | solution.py:262
  28.2 126.9 %all-gather.30.cloned.1.call-start = ((), (), s32[]{:S(2)}) async-start(), calls=%async_computation.14 | async-start | bytes 1310720 | tf_op jit(solution)/shard_map/while/body/eval_jaxpr/all_gather | solution.py:263
  28.8 211.0 %all-gather.32.cloned.1.call-start = ((), (), s32[]{:S(2)}) async-start(), calls=%async_computation.15 | async-start | bytes 1310720 | tf_op jit(solution)/shard_map/while/body/eval_jaxpr/all_gather | solution.py:270
  29.3 288.7 %reduce-scatter.12.cloned.1.call-start = ((), (), s32[]{:S(2)}) async-start(), calls=%async_computation.16 | async-start | bytes 9437184 | tf_op jit(solution)/shard_map/while/body/eval_jaxpr/reduce_scatter | solution.py:167
  247.1 153.4 %all-gather.38.cloned.1.call-start = ((), (), s32[]{:S(2)}) async-start(), calls=%async_computation.19 | async-start | bytes 5242880 | tf_op jit(solution)/shard_map/while/body/eval_jaxpr/all_gather | solution.py:271
  247.8 207.6 %all-gather.40.cloned.1.call-start = ((), (), s32[]{:S(2)}) async-start(), calls=%async_computation.20 | async-start | bytes 9437184 | tf_op jit(solution)/shard_map/while/body/eval_jaxpr/all_gather | solution.py:189
  250.2 287.6 %all-gather.36.cloned.1.call-start = ((), (), s32[]{:S(2)}) async-start(), calls=%async_computation.18 | async-start | bytes 5242880 | tf_op jit(solution)/shard_map/while/body/eval_jaxpr/all_gather | solution.py:264
  251.0 341.7 %all-gather.34.cloned.1.call-start = ((), (), s32[]{:S(2)}) async-start(), calls=%async_computation.17 | async-start | bytes 9437184 | tf_op jit(solution)/shard_map/while/body/eval_jaxpr/all_gather | solution.py:175
  263.1 537.4 %copy-start.21 = (f32[4,1,512]{2,1,0:T(1,128)}, f32[4,1,512]{2,1,0:T(1,128)S(1)}, u32[]{:S(2)}) copy-start(f32[4,1,512]{2,1,0:T(1,128)S(1)} %convert_element_type.402) | copy-start | bytes 24580 | tf_op jit(solution)/shard_map/while
  319.7 480.9 %copy-start.26 = (f32[256]{0:T(256)}, f32[256]{0:T(256)S(1)}, u32[]{:S(2)}) copy-start(f32[256]{0:T(256)S(1)} %add_rsqrt_fusion.5) | copy-start | bytes 3076 | tf_op jit(solution)/shard_map/while
  322.3 352.9 %all-gather.42.cloned.1.call-start = ((), (), s32[]{:S(2)}) async-start(), calls=%async_computation.21 | async-start | bytes 5242880 | tf_op jit(solution)/shard_map/while/body/eval_jaxpr/all_gather | solution.py:265
  323.0 474.8 %reduce-scatter.14.cloned.1.call-start = ((), (), s32[]{:S(2)}) async-start(), calls=%async_computation.22 | async-start | bytes 9437184 | tf_op jit(solution)/shard_map/while/body/eval_jaxpr/reduce_scatter | solution.py:198
  727.8 131.4 %all-gather.44.cloned.1.call-start = ((), (), s32[]{:S(2)}) async-start(), calls=%async_computation.23 | async-start | bytes 9437184 | tf_op jit(solution)/shard_map/while/body/eval_jaxpr/all_gather | solution.py:209
  804.7 395.0 %reduce-scatter.28.cloned.1.call-start = ((), (), s32[]{:S(2)}) async-start(), calls=%async_computation.30 | async-start | bytes 5242880 | tf_op jit(solution)/shard_map/while/body/eval_jaxpr/reduce_scatter | solution.py:297
  819.0 384.1 %reduce-scatter.22.cloned.1.call-start = ((), (), s32[]{:S(2)}) async-start(), calls=%async_computation.27 | async-start | bytes 5242880 | tf_op jit(solution)/shard_map/while/body/eval_jaxpr/reduce_scatter | solution.py:286
  833.1 373.9 %reduce-scatter.24.cloned.1.call-start = ((), (), s32[]{:S(2)}) async-start(), calls=%async_computation.28 | async-start | bytes 5242880 | tf_op jit(solution)/shard_map/while/body/eval_jaxpr/reduce_scatter | solution.py:289
  847.9 362.4 %reduce-scatter.26.cloned.1.call-start = ((), (), s32[]{:S(2)}) async-start(), calls=%async_computation.29 | async-start | bytes 1310720 | tf_op jit(solution)/shard_map/while/body/eval_jaxpr/reduce_scatter | solution.py:294
  875.4 336.8 %reduce-scatter.18.cloned.1.call-start = ((), (), s32[]{:S(2)}) async-start(), calls=%async_computation.25 | async-start | bytes 1310720 | tf_op jit(solution)/shard_map/while/body/eval_jaxpr/reduce_scatter | solution.py:280
  1136.2 77.8 %reduce-scatter.16.cloned.1.call-start = ((), (), s32[]{:S(2)}) async-start(), calls=%async_computation.24 | async-start | bytes 1310720 | tf_op jit(solution)/shard_map/while/body/eval_jaxpr/reduce_scatter | solution.py:277
  1143.1 76.6 %reduce-scatter.20.cloned.1.call-start = ((), (), s32[]{:S(2)}) async-start(), calls=%async_computation.26 | async-start | bytes 1310720 | tf_op jit(solution)/shard_map/while/body/eval_jaxpr/reduce_scatter | solution.py:283
  1151.8 141.7 %reduce-scatter.30.cloned.1.call-start = ((), (), s32[]{:S(2)}) async-start(), calls=%async_computation.31 | async-start | bytes 9437184 | tf_op jit(solution)/shard_map/while/body/eval_jaxpr/reduce_scatter | solution.py:221
  1185.3 183.0 %reduce-scatter.32.cloned.1.call-start = ((), (), s32[]{:S(2)}) async-start(), calls=%async_computation.32 | async-start | bytes 9437184 | tf_op jit(solution)/shard_map/while/body/eval_jaxpr/reduce_scatter | solution.py:183
  1373.9 30.4 %all-gather.28.cloned.1.call-start = ((), (), s32[]{:S(2)}) async-start(), calls=%async_computation.13 | async-start | bytes 1310720 | tf_op jit(solution)/shard_map/while/body/eval_jaxpr/all_gather | solution.py:261
  1374.7 85.3 %all-gather.24.cloned.1.call-start = ((), (), s32[]{:S(2)}) async-start(), calls=%async_computation.11 | async-start | bytes 9437184 | tf_op jit(solution)/shard_map/while/body/eval_jaxpr/all_gather | solution.py:157
  1392.0 97.5 %all-gather.26.cloned.1.call-start = ((), (), s32[]{:S(2)}) async-start(), calls=%async_computation.12 | async-start | bytes 1310720 | tf_op jit(solution)/shard_map/while/body/eval_jaxpr/all_gather | solution.py:262
  1392.8 125.6 %all-gather.30.cloned.1.call-start = ((), (), s32[]{:S(2)}) async-start(), calls=%async_computation.14 | async-start | bytes 1310720 | tf_op jit(solution)/shard_map/while/body/eval_jaxpr/all_gather | solution.py:263
  1393.3 209.8 %all-gather.32.cloned.1.call-start = ((), (), s32[]{:S(2)}) async-start(), calls=%async_computation.15 | async-start | bytes 1310720 | tf_op jit(solution)/shard_map/while/body/eval_jaxpr/all_gather | solution.py:270
  1393.9 287.4 %reduce-scatter.12.cloned.1.call-start = ((), (), s32[]{:S(2)}) async-start(), calls=%async_computation.16 | async-start | bytes 9437184 | tf_op jit(solution)/shard_map/while/body/eval_jaxpr/reduce_scatter | solution.py:167
  1610.4 153.3 %all-gather.38.cloned.1.call-start = ((), (), s32[]{:S(2)}) async-start(), calls=%async_computation.19 | async-start | bytes 5242880 | tf_op jit(solution)/shard_map/while/body/eval_jaxpr/all_gather | solution.py:271
  1611.1 207.4 %all-gather.40.cloned.1.call-start = ((), (), s32[]{:S(2)}) async-start(), calls=%async_computation.20 | async-start | bytes 9437184 | tf_op jit(solution)/shard_map/while/body/eval_jaxpr/all_gather | solution.py:189
  1613.5 287.5 %all-gather.36.cloned.1.call-start = ((), (), s32[]{:S(2)}) async-start(), calls=%async_computation.18 | async-start | bytes 5242880 | tf_op jit(solution)/shard_map/while/body/eval_jaxpr/all_gather | solution.py:264
  1614.3 341.7 %all-gather.34.cloned.1.call-start = ((), (), s32[]{:S(2)}) async-start(), calls=%async_computation.17 | async-start | bytes 9437184 | tf_op jit(solution)/shard_map/while/body/eval_jaxpr/all_gather | solution.py:175
  1626.4 537.3 %copy-start.21 = (f32[4,1,512]{2,1,0:T(1,128)}, f32[4,1,512]{2,1,0:T(1,128)S(1)}, u32[]{:S(2)}) copy-start(f32[4,1,512]{2,1,0:T(1,128)S(1)} %convert_element_type.402) | copy-start | bytes 24580 | tf_op jit(solution)/shard_map/while
  1683.0 480.8 %copy-start.26 = (f32[256]{0:T(256)}, f32[256]{0:T(256)S(1)}, u32[]{:S(2)}) copy-start(f32[256]{0:T(256)S(1)} %add_rsqrt_fusion.5) | copy-start | bytes 3076 | tf_op jit(solution)/shard_map/while
  1685.6 352.8 %all-gather.42.cloned.1.call-start = ((), (), s32[]{:S(2)}) async-start(), calls=%async_computation.21 | async-start | bytes 5242880 | tf_op jit(solution)/shard_map/while/body/eval_jaxpr/all_gather | solution.py:265
  1686.2 474.8 %reduce-scatter.14.cloned.1.call-start = ((), (), s32[]{:S(2)}) async-start(), calls=%async_computation.22 | async-start | bytes 9437184 | tf_op jit(solution)/shard_map/while/body/eval_jaxpr/reduce_scatter | solution.py:198
  2091.0 131.4 %all-gather.44.cloned.1.call-start = ((), (), s32[]{:S(2)}) async-start(), calls=%async_computation.23 | async-start | bytes 9437184 | tf_op jit(solution)/shard_map/while/body/eval_jaxpr/all_gather | solution.py:209
  2167.9 395.0 %reduce-scatter.28.cloned.1.call-start = ((), (), s32[]{:S(2)}) async-start(), calls=%async_computation.30 | async-start | bytes 5242880 | tf_op jit(solution)/shard_map/while/body/eval_jaxpr/reduce_scatter | solution.py:297
  2182.2 384.1 %reduce-scatter.22.cloned.1.call-start = ((), (), s32[]{:S(2)}) async-start(), calls=%async_computation.27 | async-start | bytes 5242880 | tf_op jit(solution)/shard_map/while/body/eval_jaxpr/reduce_scatter | solution.py:286
  2196.3 374.5 %reduce-scatter.24.cloned.1.call-start = ((), (), s32[]{:S(2)}) async-start(), calls=%async_computation.28 | async-start | bytes 5242880 | tf_op jit(solution)/shard_map/while/body/eval_jaxpr/reduce_scatter | solution.py:289
  2211.0 363.7 %reduce-scatter.26.cloned.1.call-start = ((), (), s32[]{:S(2)}) async-start(), calls=%async_computation.29 | async-start | bytes 1310720 | tf_op jit(solution)/shard_map/while/body/eval_jaxpr/reduce_scatter | solution.py:294
  2238.5 338.2 %reduce-scatter.18.cloned.1.call-start = ((), (), s32[]{:S(2)}) async-start(), calls=%async_computation.25 | async-start | bytes 1310720 | tf_op jit(solution)/shard_map/while/body/eval_jaxpr/reduce_scatter | solution.py:280
  2499.3 79.4 %reduce-scatter.16.cloned.1.call-start = ((), (), s32[]{:S(2)}) async-start(), calls=%async_computation.24 | async-start | bytes 1310720 | tf_op jit(solution)/shard_map/while/body/eval_jaxpr/reduce_scatter | solution.py:277
  2506.2 76.8 %reduce-scatter.20.cloned.1.call-start = ((), (), s32[]{:S(2)}) async-start(), calls=%async_computation.26 | async-start | bytes 1310720 | tf_op jit(solution)/shard_map/while/body/eval_jaxpr/reduce_scatter | solution.py:283
  2514.9 141.8 %reduce-scatter.30.cloned.1.call-start = ((), (), s32[]{:S(2)}) async-start(), calls=%async_computation.31 | async-start | bytes 9437184 | tf_op jit(solution)/shard_map/while/body/eval_jaxpr/reduce_scatter | solution.py:221
  2548.4 183.1 %reduce-scatter.32.cloned.1.call-start = ((), (), s32[]{:S(2)}) async-start(), calls=%async_computation.32 | async-start | bytes 9437184 | tf_op jit(solution)/shard_map/while/body/eval_jaxpr/reduce_scatter | solution.py:183
  (104 other events, 3378.5 us)
Sparse Core Ops, SparseCore 0:
  10.2 30.6 all-gather.27
  42.7 53.8 all-gather.23
  98.2 27.9 all-gather.25
  127.6 27.4 all-gather.29
  156.5 27.4 all-gather.31
  247.2 70.7 reduce-scatter.11
  319.6 80.7 all-gather.37
  402.5 52.9 all-gather.39
  457.1 80.7 all-gather.35
  539.8 52.9 all-gather.33
  594.4 80.7 all-gather.41
  727.9 69.8 reduce-scatter.13
  804.8 54.3 all-gather.43
  861.4 76.7 reduce-scatter.27
  940.4 77.2 reduce-scatter.21
  1019.9 77.2 reduce-scatter.23
  1099.4 27.6 reduce-scatter.25
  1136.3 27.2 reduce-scatter.17
  1165.9 25.7 reduce-scatter.15
  1193.9 25.7 reduce-scatter.19
  1223.6 69.9 reduce-scatter.29
  1297.0 71.2 reduce-scatter.31
  1376.3 27.9 all-gather.27
  1406.0 53.8 all-gather.23
  1461.5 27.9 all-gather.25
  1490.9 27.4 all-gather.29
  1519.8 27.4 all-gather.31
  1610.5 70.7 reduce-scatter.11
  1683.0 80.7 all-gather.37
  1765.6 52.9 all-gather.39
  1820.2 80.7 all-gather.35
  1903.1 52.9 all-gather.33
  1957.5 80.7 all-gather.41
  2091.1 69.8 reduce-scatter.13
  2168.0 54.3 all-gather.43
  2224.5 76.7 reduce-scatter.27
  2303.6 77.2 reduce-scatter.21
  2383.2 77.2 reduce-scatter.23
  2462.7 27.6 reduce-scatter.25
  2499.4 27.3 reduce-scatter.17
  2529.1 25.7 reduce-scatter.15
  2557.2 25.7 reduce-scatter.19
  2586.7 69.9 reduce-scatter.29
  2660.2 71.2 reduce-scatter.31
where the time goes:
time: 2790 us
  waiting for transfers between devices  1440 us (52%)
  matrix products  787 us (28%)
  other arithmetic  254 us (9%)
  local copies, waits for them, and re-layouts  161 us (6%)
  blocking collectives  89.3 us (3%)
  loops' own time  37.8 us (1%)
    dot_general x14, matrix products, mat_back(): lax.dot_general(left_op, right_op, (((1,), (1,)), ((), ())), preferred_el...  169 us
    all_gather x2, waiting for transfers between devices, fetch_weights(): lax.all_gather(w_down, 'narrow', axis=1, tiled=True)  155 us
    dot_general x14, matrix products, mat_plain(): return jnp.dot(left_op, right_op, preferred_element_type=jnp.float32)  151 us
    reduce_scatter x2, waiting for transfers between devices, one_row(): lax.psum_scatter(rounded(mat_plain(hidden, w_down)).astype(jnp.bfloat16),...  145 us
    reduce_scatter x2, waiting for transfers between devices, one_row(): lax.psum_scatter(rounded(mat_back(query_raw, w_query) + mat_back(key_raw,...  144 us
    reduce_scatter x2, waiting for transfers between devices, one_row(): lax.psum_scatter(rounded(mat_back(grad_gate_pre, w_gate) + mat_back(grad_...  140 us
    all_gather x2, waiting for transfers between devices, fetch_weights(): lax.all_gather(w_up, 'narrow', axis=0, tiled=True)  136 us
    all_gather x2, waiting for transfers between devices, fetch_weights(): lax.all_gather(w_gate, 'narrow', axis=0, tiled=True)  135 us
  transfers between devices with their start and end apart: 44, of which 30 were waited for; matrix products, arithmetic and copies ran while one was open for 38% of the time, Pallas kernels for 0%

commit v1 on v0

--- a/solution.py
+++ b/solution.py
@@ -186,7 +186,12 @@
         scatter_dimension=0,
         tiled=True,
     ).astype(jnp.float32)
-    grad_full = lax.all_gather(grad_row, "wide", axis=0, tiled=True)
+    ring = [grad_row]
+    for hop in range(7):
+        ring.append(lax.ppermute(ring[-1], "wide", [(dev, (dev + 1) % 8) for dev in range(8)]))
+    grad_full = jnp.roll(
+        jnp.concatenate(ring[::-1], axis=0), (lax.axis_index("wide") + 1) * ring[0].shape[0], axis=0
+    )
     grad_down = mat_outer(hidden, grad_full)
     grad_hidden = mat_back(grad_full, w_down)
     grad_gate_pre = (

time: 2790 us -> 2720 us (0.975)
  waiting for transfers between devices: 1440 us -> 1310 us
  local copies, waits for them, and re-layouts: 161 us -> 214 us
    ppermute x0 -> x14, waiting for transfers between devices: none -> 272 us  [one_row(): lax.ppermute(ring[-1], 'wide', [(dev, (dev + 1) % 8) for dev in range(8)])]
    all_gather x2, waiting for transfers between devices: 135 us -> 0.01 us  [fetch_weights(): lax.all_gather(w_gate, 'narrow', axis=0, tiled=True)]
    all_gather x2, waiting for transfers between devices: 110 us -> 0.01 us  [one_row(): lax.all_gather((normed_mid * mlp_scale).astype(jnp.bfloat16), 'wide', axi...]
    all_gather x2 -> x0, waiting for transfers between devices: 110 us -> none  [one_row(): grad_full = lax.all_gather(grad_row, 'wide', axis=0, tiled=True)]
    while x226 -> x292, local copies, waits for them, and re-layouts: 20 us -> 70.5 us
    all_gather x2, waiting for transfers between devices: 136 us -> 103 us  [fetch_weights(): lax.all_gather(w_up, 'narrow', axis=0, tiled=True)]
  transfers between devices with their start and end apart: 44 -> 56, of which waited for: 30 -> 38; matrix products, arithmetic and copies ran while one was open for 38% -> 40% of each run, Pallas kernels for 0% -> 0%
where the time goes in v1:
time: 2720 us; the launch traced here: 2710 us
  waiting for transfers between devices  1310 us (48%)
  matrix products  793 us (29%)
  other arithmetic  255 us (9%)
  local copies, waits for them, and re-layouts  214 us (8%)
  blocking collectives  89.3 us (3%)
  loops' own time  37.8 us (1%)
    ppermute x14, waiting for transfers between devices, one_row(): lax.ppermute(ring[-1], 'wide', [(dev, (dev + 1) % 8) for dev in range(8)])  272 us
    dot_general x14, matrix products, mat_back(): lax.dot_general(left_op, right_op, (((1,), (1,)), ((), ())), preferred_el...  189 us
    reduce_scatter x2, waiting for transfers between devices, one_row(): lax.psum_scatter(rounded(mat_plain(hidden, w_down)).astype(jnp.bfloat16),...  145 us
    reduce_scatter x2, waiting for transfers between devices, one_row(): lax.psum_scatter(rounded(mat_back(query_raw, w_query) + mat_back(key_raw,...  144 us
    reduce_scatter x2, waiting for transfers between devices, one_row(): lax.psum_scatter(rounded(mat_back(grad_gate_pre, w_gate) + mat_back(grad_...  140 us
    dot_general x14, matrix products, mat_plain(): return jnp.dot(left_op, right_op, preferred_element_type=jnp.float32)  136 us
    dot_general x14, matrix products, mat_outer(): lax.dot_general(left_op, right_op, (((0,), (0,)), ((), ())), preferred_el...  135 us
    all_gather x2, waiting for transfers between devices, fetch_weights(): lax.all_gather(w_down, 'narrow', axis=1, tiled=True)  133 us
  transfers between devices with their start and end apart: 56, of which 38 were waited for; matrix products, arithmetic and copies ran while one was open for 40% of the time, Pallas kernels for 0%

profile of v1, /device:TPU:0, one launch (start us, length us, event | category | flops | bytes accessed | tf_op | source)
XLA Modules:
  0.0 2711.5 jit_solution(15680011454860442477)
XLA Ops:
  7.3 2656.5 %while.91 = (s32[]{:T(128)}, f32[512,256]{1,0:T(8,128)}, f32[512,256]{1,0:T(8,128)}, f32[512,256]{1,0:T(8,128)}, f32[512,1024]{1,0:T(8,128)}, /*index=5*/f32[512...) while((s32[]{:T(128)}, f32[512,256]{1,0:T(8,128)}, ...), condition=%wide.region_27.28_spmd.clone, body=%wide.region_0.27_spmd.clone.sunk | while | flops 107088232448 | bytes 1288338432 | solution.py:330
  40.8 55.8 %all-gather.19.cloned.1.call-done = bf16[2048,2048]{1,0:T(8,128)(2,1)} async-done(((bf16[256,2048]{1,0:T(8,128)(2,1)}), bf16[2048,2048]{1,0:T(8,128)(2,1)}) %all-gather.19.cloned.1.call-update) | async-done | bytes 8388624 | tf_op jit(solution)/shard_map/while/body/eval_jaxpr/all_gather | solution.py:157
  102.6 23.6 all-gather.21.cloned.1.call-done
  133.0 22.1 all-gather.25.cloned.1.call-done
  161.1 74.7 %while.92 = (s32[]{:T(128)}, bf16[4,512,4,64]{1,3,2,0:T(8,128)(2,1)}, f32[4,4,512]{2,1,0:T(4,128)}, s32[4]{0:T(128)S(1)}, s32[2048]{0:T(1024)}, /*index=5*/bf16[...) while((s32[]{:T(128)}, ...), condition=%wide.region_7.7_spmd, body=%wide.region_4.6_spmd.sunk | while | flops 1127217664 | bytes 65874156 | solution.py:91
  260.1 58.0 %reduce-scatter.12.cloned.1.call-done = bf16[256,2048]{1,0:T(8,128)(2,1)} async-done(((bf16[2048,2048]{1,0:T(8,128)(2,1)}), bf16[256,2048]{1,0:T(8,128)(2,1)}) %reduce-scatter.12.cloned.1.call-update) | async-done | bytes 1048592 | tf_op jit(solution)/shard_map/while/body/eval_jaxpr/reduce_scatter | solution.py:167
  324.9 15.3 collective-permute-done
  340.2 15.1 collective-permute-done.1
  356.3 15.1 collective-permute-done.2
  372.4 15.1 collective-permute-done.3
  388.5 15.1 collective-permute-done.4
  404.6 26.5 collective-permute-done.5
  431.2 33.7 %collective-permute-done.6 = bf16[256,2048]{1,0:T(8,128)(2,1)} collective-permute-done((bf16[256,2048]{1,0:T(8,128)(2,1)}, bf16[256,2048]{1,0:T(8,128)(2,1)}, u32[]{:S(2)}, u32[]{:S(2)}) %collective-permute-start.6) | collective-permute-done | bytes 1048608 | tf_op jit(solution)/shard_map/while/body/eval_jaxpr/ppermute | solution.py:191
  501.7 51.6 %all-gather.31.cloned.1.call-done = bf16[2048,1024]{1,0:T(8,128)(2,1)} async-done(((bf16[512,1024]{1,0:T(8,128)(2,1)}), bf16[2048,1024]{1,0:T(8,128)(2,1)}) %all-gather.31.cloned.1.call-update) | async-done | bytes 4194320 | tf_op jit(solution)/shard_map/while/body/eval_jaxpr/all_gather | solution.py:270
  567.7 66.4 %all-gather.35.cloned.1.call-done = bf16[1024,2048]{1,0:T(8,128)(2,1)} async-done(((bf16[1024,512]{1,0:T(8,128)(2,1)}), bf16[1024,2048]{1,0:T(8,128)(2,1)}) %all-gather.35.cloned.1.call-update) | async-done | bytes 4194320 | tf_op jit(solution)/shard_map/while/body/eval_jaxpr/all_gather | solution.py:276
  634.1 24.1 multiply_convert_fusion.9
  658.2 15.5 fusion.258
  673.6 16.0 add_convert_fusion.9
  689.8 70.0 %reduce-scatter.14.cloned.1.call-done = bf16[256,2048]{1,0:T(8,128)(2,1)} async-done(((bf16[2048,2048]{1,0:T(8,128)(2,1)}), bf16[256,2048]{1,0:T(8,128)(2,1)}) %reduce-scatter.14.cloned.1.call-update) | async-done | bytes 1048592 | tf_op jit(solution)/shard_map/while/body/eval_jaxpr/reduce_scatter | solution.py:203
  795.3 14.6 convolution_convert_fusion.27
  837.3 249.8 %while.93 = (s32[]{:T(128)}, f32[2048,4,64]{0,2,1:T(8,128)}, f32[2048,4,64]{0,2,1:T(8,128)}, f32[4,512,4,64]{1,0,3,2:T(4,128)}, bf16[4,512,4,64]{1,3,2,0:T(8,128...) while((s32[]{:T(128)}, f32[2048,4,64]{0,2,1:T(8,128)}, ...), condition=%wide.region_14.14_spmd.clone, body=%wide.region_12.13_spmd.clone.sunk | while | flops 2753165824 | bytes 183044368 | solution.py:134
  1132.3 15.6 add_convert_fusion.10
  1184.1 71.9 %reduce-scatter.30.cloned.1.call-done = bf16[256,2048]{1,0:T(8,128)(2,1)} async-done(((bf16[2048,2048]{1,0:T(8,128)(2,1)}), bf16[256,2048]{1,0:T(8,128)(2,1)}) %reduce-scatter.30.cloned.1.call-update) | async-done | bytes 1048592 | tf_op jit(solution)/shard_map/while/body/eval_jaxpr/reduce_scatter | solution.py:226
  1258.0 72.7 %reduce-scatter.32.cloned.1.call-done = bf16[256,2048]{1,0:T(8,128)(2,1)} async-done(((bf16[2048,2048]{1,0:T(8,128)(2,1)}), bf16[256,2048]{1,0:T(8,128)(2,1)}) %reduce-scatter.32.cloned.1.call-update) | async-done | bytes 1048592 | tf_op jit(solution)/shard_map/while/body/eval_jaxpr/reduce_scatter | solution.py:183
  1366.6 55.8 %all-gather.19.cloned.1.call-done = bf16[2048,2048]{1,0:T(8,128)(2,1)} async-done(((bf16[256,2048]{1,0:T(8,128)(2,1)}), bf16[2048,2048]{1,0:T(8,128)(2,1)}) %all-gather.19.cloned.1.call-update) | async-done | bytes 8388624 | tf_op jit(solution)/shard_map/while/body/eval_jaxpr/all_gather | solution.py:157
  1428.4 23.4 all-gather.21.cloned.1.call-done
  1458.6 22.2 all-gather.25.cloned.1.call-done
  1486.8 75.0 %while.92 = (s32[]{:T(128)}, bf16[4,512,4,64]{1,3,2,0:T(8,128)(2,1)}, f32[4,4,512]{2,1,0:T(4,128)}, s32[4]{0:T(128)S(1)}, s32[2048]{0:T(1024)}, /*index=5*/bf16[...) while((s32[]{:T(128)}, ...), condition=%wide.region_7.7_spmd, body=%wide.region_4.6_spmd.sunk | while | flops 1127217664 | bytes 65874156 | solution.py:91
  1586.1 58.0 %reduce-scatter.12.cloned.1.call-done = bf16[256,2048]{1,0:T(8,128)(2,1)} async-done(((bf16[2048,2048]{1,0:T(8,128)(2,1)}), bf16[256,2048]{1,0:T(8,128)(2,1)}) %reduce-scatter.12.cloned.1.call-update) | async-done | bytes 1048592 | tf_op jit(solution)/shard_map/while/body/eval_jaxpr/reduce_scatter | solution.py:167
  1650.9 15.3 collective-permute-done
  1666.2 15.1 collective-permute-done.1
  1682.3 15.1 collective-permute-done.2
  1698.4 15.1 collective-permute-done.3
  1714.5 15.1 collective-permute-done.4
  1730.6 26.5 collective-permute-done.5
  1757.2 33.7 %collective-permute-done.6 = bf16[256,2048]{1,0:T(8,128)(2,1)} collective-permute-done((bf16[256,2048]{1,0:T(8,128)(2,1)}, bf16[256,2048]{1,0:T(8,128)(2,1)}, u32[]{:S(2)}, u32[]{:S(2)}) %collective-permute-start.6) | collective-permute-done | bytes 1048608 | tf_op jit(solution)/shard_map/while/body/eval_jaxpr/ppermute | solution.py:191
  1827.7 51.4 %all-gather.31.cloned.1.call-done = bf16[2048,1024]{1,0:T(8,128)(2,1)} async-done(((bf16[512,1024]{1,0:T(8,128)(2,1)}), bf16[2048,1024]{1,0:T(8,128)(2,1)}) %all-gather.31.cloned.1.call-update) | async-done | bytes 4194320 | tf_op jit(solution)/shard_map/while/body/eval_jaxpr/all_gather | solution.py:270
  1893.6 66.5 %all-gather.35.cloned.1.call-done = bf16[1024,2048]{1,0:T(8,128)(2,1)} async-done(((bf16[1024,512]{1,0:T(8,128)(2,1)}), bf16[1024,2048]{1,0:T(8,128)(2,1)}) %all-gather.35.cloned.1.call-update) | async-done | bytes 4194320 | tf_op jit(solution)/shard_map/while/body/eval_jaxpr/all_gather | solution.py:276
  1960.1 23.9 multiply_convert_fusion.9
  1983.9 15.5 fusion.258
  1999.4 16.3 add_convert_fusion.9
  2015.8 70.0 %reduce-scatter.14.cloned.1.call-done = bf16[256,2048]{1,0:T(8,128)(2,1)} async-done(((bf16[2048,2048]{1,0:T(8,128)(2,1)}), bf16[256,2048]{1,0:T(8,128)(2,1)}) %reduce-scatter.14.cloned.1.call-update) | async-done | bytes 1048592 | tf_op jit(solution)/shard_map/while/body/eval_jaxpr/reduce_scatter | solution.py:203
  2121.1 14.7 convolution_convert_fusion.27
  2163.4 249.8 %while.93 = (s32[]{:T(128)}, f32[2048,4,64]{0,2,1:T(8,128)}, f32[2048,4,64]{0,2,1:T(8,128)}, f32[4,512,4,64]{1,0,3,2:T(4,128)}, bf16[4,512,4,64]{1,3,2,0:T(8,128...) while((s32[]{:T(128)}, f32[2048,4,64]{0,2,1:T(8,128)}, ...), condition=%wide.region_14.14_spmd.clone, body=%wide.region_12.13_spmd.clone.sunk | while | flops 2753165824 | bytes 183044368 | solution.py:134
  2458.2 15.6 add_convert_fusion.10
  2510.3 71.9 %reduce-scatter.30.cloned.1.call-done = bf16[256,2048]{1,0:T(8,128)(2,1)} async-done(((bf16[2048,2048]{1,0:T(8,128)(2,1)}), bf16[256,2048]{1,0:T(8,128)(2,1)}) %reduce-scatter.30.cloned.1.call-update) | async-done | bytes 1048592 | tf_op jit(solution)/shard_map/while/body/eval_jaxpr/reduce_scatter | solution.py:226
  2584.2 72.7 %reduce-scatter.32.cloned.1.call-done = bf16[256,2048]{1,0:T(8,128)(2,1)} async-done(((bf16[2048,2048]{1,0:T(8,128)(2,1)}), bf16[256,2048]{1,0:T(8,128)(2,1)}) %reduce-scatter.32.cloned.1.call-update) | async-done | bytes 1048592 | tf_op jit(solution)/shard_map/while/body/eval_jaxpr/reduce_scatter | solution.py:183
  2663.8 39.7 %all-reduce.2 = (f32[2048]{0:T(1024)S(1)}, f32[2048]{0:T(1024)S(1)}) all-reduce(f32[2048]{0:T(1024)} %get-tuple-element.420, f32[2048]{0:T(1024)} %get-tuple-element.425), channel_id=13, replica_groups=mesh['narrow'=4,'wide'=8] {'narrow','wide'}, use_global_device_ids=true, to_apply=%region_28.29.clone | all-reduce | flops 4096 | bytes 32768
  (723 shorter events, 1192.4 us)
Async XLA Ops:
  7.8 33.1 %all-gather.23.cloned.1.call-start = ((), (), s32[]{:S(2)}) async-start(), calls=%async_computation.13 | async-start | bytes 1310720 | tf_op jit(solution)/shard_map/while/body/eval_jaxpr/all_gather | solution.py:266
  8.5 88.1 %all-gather.19.cloned.1.call-start = ((), (), s32[]{:S(2)}) async-start(), calls=%async_computation.11 | async-start | bytes 9437184 | tf_op jit(solution)/shard_map/while/body/eval_jaxpr/all_gather | solution.py:157
  27.5 98.7 %all-gather.21.cloned.1.call-start = ((), (), s32[]{:S(2)}) async-start(), calls=%async_computation.12 | async-start | bytes 1310720 | tf_op jit(solution)/shard_map/while/body/eval_jaxpr/all_gather | solution.py:267
  28.2 126.9 %all-gather.25.cloned.1.call-start = ((), (), s32[]{:S(2)}) async-start(), calls=%async_computation.14 | async-start | bytes 1310720 | tf_op jit(solution)/shard_map/while/body/eval_jaxpr/all_gather | solution.py:268
  28.8 211.1 %all-gather.27.cloned.1.call-start = ((), (), s32[]{:S(2)}) async-start(), calls=%async_computation.15 | async-start | bytes 1310720 | tf_op jit(solution)/shard_map/while/body/eval_jaxpr/all_gather | solution.py:275
  29.4 288.7 %reduce-scatter.12.cloned.1.call-start = ((), (), s32[]{:S(2)}) async-start(), calls=%async_computation.16 | async-start | bytes 9437184 | tf_op jit(solution)/shard_map/while/body/eval_jaxpr/reduce_scatter | solution.py:167
  247.2 240.0 %all-gather.33.cloned.1.call-start = ((), (), s32[]{:S(2)}) async-start(), calls=%async_computation.19 | async-start | bytes 5242880 | tf_op jit(solution)/shard_map/while/body/eval_jaxpr/all_gather | solution.py:269
  248.0 239.3 %all-gather.29.cloned.1.call-start = ((), (), s32[]{:S(2)}) async-start(), calls=%async_computation.17 | async-start | bytes 9437184 | tf_op jit(solution)/shard_map/while/body/eval_jaxpr/all_gather | solution.py:175
  322.4 230.9 %all-gather.31.cloned.1.call-start = ((), (), s32[]{:S(2)}) async-start(), calls=%async_computation.18 | async-start | bytes 5242880 | tf_op jit(solution)/shard_map/while/body/eval_jaxpr/all_gather | solution.py:270
  324.8 15.3 collective-permute-start
  324.9 309.3 %all-gather.35.cloned.1.call-start = ((), (), s32[]{:S(2)}) async-start(), calls=%async_computation.20 | async-start | bytes 5242880 | tf_op jit(solution)/shard_map/while/body/eval_jaxpr/all_gather | solution.py:276
  404.6 26.5 collective-permute-start.5
  431.1 33.9 %collective-permute-start.6 = (bf16[256,2048]{1,0:T(8,128)(2,1)}, bf16[256,2048]{1,0:T(8,128)(2,1)}, u32[]{:S(2)}, u32[]{:S(2)}) collective-permute-start(bf16[256,2048]{1,0:T(8,128)(2,1)} %collective-permute-done.5), channel_id=1, source_target_pairs={{0,1},{1,2},{2,3},{3,4},{4,5},{5,6},{6,7},{7,0},{8,9},{9,10},{10,1... | collective-permute-start | bytes 3145736 | tf_op jit(solution)/shard_map/while/body/eval_jaxpr/ppermute | solution.py:191
  431.1 328.6 %reduce-scatter.14.cloned.1.call-start = ((), (), s32[]{:S(2)}) async-start(), calls=%async_computation.21 | async-start | bytes 9437184 | tf_op jit(solution)/shard_map/while/body/eval_jaxpr/reduce_scatter | solution.py:203
  689.7 131.5 %all-gather.37.cloned.1.call-start = ((), (), s32[]{:S(2)}) async-start(), calls=%async_computation.22 | async-start | bytes 9437184 | tf_op jit(solution)/shard_map/while/body/eval_jaxpr/all_gather | solution.py:214
  766.6 395.6 %reduce-scatter.28.cloned.1.call-start = ((), (), s32[]{:S(2)}) async-start(), calls=%async_computation.29 | async-start | bytes 5242880 | tf_op jit(solution)/shard_map/while/body/eval_jaxpr/reduce_scatter | solution.py:302
  780.7 384.9 %reduce-scatter.22.cloned.1.call-start = ((), (), s32[]{:S(2)}) async-start(), calls=%async_computation.26 | async-start | bytes 5242880 | tf_op jit(solution)/shard_map/while/body/eval_jaxpr/reduce_scatter | solution.py:291
  795.3 374.2 %reduce-scatter.24.cloned.1.call-start = ((), (), s32[]{:S(2)}) async-start(), calls=%async_computation.27 | async-start | bytes 5242880 | tf_op jit(solution)/shard_map/while/body/eval_jaxpr/reduce_scatter | solution.py:294
  809.9 362.9 %reduce-scatter.26.cloned.1.call-start = ((), (), s32[]{:S(2)}) async-start(), calls=%async_computation.28 | async-start | bytes 1310720 | tf_op jit(solution)/shard_map/while/body/eval_jaxpr/reduce_scatter | solution.py:299
  837.3 337.4 %reduce-scatter.18.cloned.1.call-start = ((), (), s32[]{:S(2)}) async-start(), calls=%async_computation.24 | async-start | bytes 1310720 | tf_op jit(solution)/shard_map/while/body/eval_jaxpr/reduce_scatter | solution.py:285
  1098.8 77.7 %reduce-scatter.16.cloned.1.call-start = ((), (), s32[]{:S(2)}) async-start(), calls=%async_computation.23 | async-start | bytes 1310720 | tf_op jit(solution)/shard_map/while/body/eval_jaxpr/reduce_scatter | solution.py:282
  1105.8 76.5 %reduce-scatter.20.cloned.1.call-start = ((), (), s32[]{:S(2)}) async-start(), calls=%async_computation.25 | async-start | bytes 1310720 | tf_op jit(solution)/shard_map/while/body/eval_jaxpr/reduce_scatter | solution.py:288
  1114.5 141.5 %reduce-scatter.30.cloned.1.call-start = ((), (), s32[]{:S(2)}) async-start(), calls=%async_computation.30 | async-start | bytes 9437184 | tf_op jit(solution)/shard_map/while/body/eval_jaxpr/reduce_scatter | solution.py:226
  1147.9 182.8 %reduce-scatter.32.cloned.1.call-start = ((), (), s32[]{:S(2)}) async-start(), calls=%async_computation.31 | async-start | bytes 9437184 | tf_op jit(solution)/shard_map/while/body/eval_jaxpr/reduce_scatter | solution.py:183
  1336.2 30.4 %all-gather.23.cloned.1.call-start = ((), (), s32[]{:S(2)}) async-start(), calls=%async_computation.13 | async-start | bytes 1310720 | tf_op jit(solution)/shard_map/while/body/eval_jaxpr/all_gather | solution.py:266
  1337.0 85.4 %all-gather.19.cloned.1.call-start = ((), (), s32[]{:S(2)}) async-start(), calls=%async_computation.11 | async-start | bytes 9437184 | tf_op jit(solution)/shard_map/while/body/eval_jaxpr/all_gather | solution.py:157
  1354.3 97.5 %all-gather.21.cloned.1.call-start = ((), (), s32[]{:S(2)}) async-start(), calls=%async_computation.12 | async-start | bytes 1310720 | tf_op jit(solution)/shard_map/while/body/eval_jaxpr/all_gather | solution.py:267
  1354.9 125.9 %all-gather.25.cloned.1.call-start = ((), (), s32[]{:S(2)}) async-start(), calls=%async_computation.14 | async-start | bytes 1310720 | tf_op jit(solution)/shard_map/while/body/eval_jaxpr/all_gather | solution.py:268
  1355.6 210.2 %all-gather.27.cloned.1.call-start = ((), (), s32[]{:S(2)}) async-start(), calls=%async_computation.15 | async-start | bytes 1310720 | tf_op jit(solution)/shard_map/while/body/eval_jaxpr/all_gather | solution.py:275
  1356.2 287.9 %reduce-scatter.12.cloned.1.call-start = ((), (), s32[]{:S(2)}) async-start(), calls=%async_computation.16 | async-start | bytes 9437184 | tf_op jit(solution)/shard_map/while/body/eval_jaxpr/reduce_scatter | solution.py:167
  1573.2 240.1 %all-gather.33.cloned.1.call-start = ((), (), s32[]{:S(2)}) async-start(), calls=%async_computation.19 | async-start | bytes 5242880 | tf_op jit(solution)/shard_map/while/body/eval_jaxpr/all_gather | solution.py:269
  1573.9 239.3 %all-gather.29.cloned.1.call-start = ((), (), s32[]{:S(2)}) async-start(), calls=%async_computation.17 | async-start | bytes 9437184 | tf_op jit(solution)/shard_map/while/body/eval_jaxpr/all_gather | solution.py:175
  1648.4 230.7 %all-gather.31.cloned.1.call-start = ((), (), s32[]{:S(2)}) async-start(), calls=%async_computation.18 | async-start | bytes 5242880 | tf_op jit(solution)/shard_map/while/body/eval_jaxpr/all_gather | solution.py:270
  1650.8 15.3 collective-permute-start
  1650.8 309.2 %all-gather.35.cloned.1.call-start = ((), (), s32[]{:S(2)}) async-start(), calls=%async_computation.20 | async-start | bytes 5242880 | tf_op jit(solution)/shard_map/while/body/eval_jaxpr/all_gather | solution.py:276
  1730.6 26.5 collective-permute-start.5
  1757.1 33.9 %collective-permute-start.6 = (bf16[256,2048]{1,0:T(8,128)(2,1)}, bf16[256,2048]{1,0:T(8,128)(2,1)}, u32[]{:S(2)}, u32[]{:S(2)}) collective-permute-start(bf16[256,2048]{1,0:T(8,128)(2,1)} %collective-permute-done.5), channel_id=1, source_target_pairs={{0,1},{1,2},{2,3},{3,4},{4,5},{5,6},{6,7},{7,0},{8,9},{9,10},{10,1... | collective-permute-start | bytes 3145736 | tf_op jit(solution)/shard_map/while/body/eval_jaxpr/ppermute | solution.py:191
  1757.1 328.6 %reduce-scatter.14.cloned.1.call-start = ((), (), s32[]{:S(2)}) async-start(), calls=%async_computation.21 | async-start | bytes 9437184 | tf_op jit(solution)/shard_map/while/body/eval_jaxpr/reduce_scatter | solution.py:203
  2015.7 131.5 %all-gather.37.cloned.1.call-start = ((), (), s32[]{:S(2)}) async-start(), calls=%async_computation.22 | async-start | bytes 9437184 | tf_op jit(solution)/shard_map/while/body/eval_jaxpr/all_gather | solution.py:214
  2092.6 395.6 %reduce-scatter.28.cloned.1.call-start = ((), (), s32[]{:S(2)}) async-start(), calls=%async_computation.29 | async-start | bytes 5242880 | tf_op jit(solution)/shard_map/while/body/eval_jaxpr/reduce_scatter | solution.py:302
  2106.7 385.0 %reduce-scatter.22.cloned.1.call-start = ((), (), s32[]{:S(2)}) async-start(), calls=%async_computation.26 | async-start | bytes 5242880 | tf_op jit(solution)/shard_map/while/body/eval_jaxpr/reduce_scatter | solution.py:291
  2121.0 375.1 %reduce-scatter.24.cloned.1.call-start = ((), (), s32[]{:S(2)}) async-start(), calls=%async_computation.27 | async-start | bytes 5242880 | tf_op jit(solution)/shard_map/while/body/eval_jaxpr/reduce_scatter | solution.py:294
  2135.7 364.3 %reduce-scatter.26.cloned.1.call-start = ((), (), s32[]{:S(2)}) async-start(), calls=%async_computation.28 | async-start | bytes 1310720 | tf_op jit(solution)/shard_map/while/body/eval_jaxpr/reduce_scatter | solution.py:299
  2163.3 338.9 %reduce-scatter.18.cloned.1.call-start = ((), (), s32[]{:S(2)}) async-start(), calls=%async_computation.24 | async-start | bytes 1310720 | tf_op jit(solution)/shard_map/while/body/eval_jaxpr/reduce_scatter | solution.py:285
  2424.8 79.4 %reduce-scatter.16.cloned.1.call-start = ((), (), s32[]{:S(2)}) async-start(), calls=%async_computation.23 | async-start | bytes 1310720 | tf_op jit(solution)/shard_map/while/body/eval_jaxpr/reduce_scatter | solution.py:282
  2431.8 76.5 %reduce-scatter.20.cloned.1.call-start = ((), (), s32[]{:S(2)}) async-start(), calls=%async_computation.25 | async-start | bytes 1310720 | tf_op jit(solution)/shard_map/while/body/eval_jaxpr/reduce_scatter | solution.py:288
  2440.5 141.7 %reduce-scatter.30.cloned.1.call-start = ((), (), s32[]{:S(2)}) async-start(), calls=%async_computation.30 | async-start | bytes 9437184 | tf_op jit(solution)/shard_map/while/body/eval_jaxpr/reduce_scatter | solution.py:226
  2473.9 183.0 %reduce-scatter.32.cloned.1.call-start = ((), (), s32[]{:S(2)}) async-start(), calls=%async_computation.31 | async-start | bytes 9437184 | tf_op jit(solution)/shard_map/while/body/eval_jaxpr/reduce_scatter | solution.py:183
  (134 other events, 5636.1 us)
Sparse Core Ops, SparseCore 0:
  10.2 30.6 all-gather.22
  42.7 53.8 all-gather.18
  98.2 27.9 all-gather.20
  127.6 27.4 all-gather.24
  156.5 27.4 all-gather.26
  247.3 70.7 reduce-scatter.11
  319.8 80.7 all-gather.32
  402.6 68.2 all-gather.28
  472.6 80.6 all-gather.30
  554.8 79.2 all-gather.34
  689.8 69.8 reduce-scatter.13
  766.8 54.3 all-gather.36
  823.5 76.8 reduce-scatter.27
  902.6 77.1 reduce-scatter.21
  981.9 77.2 reduce-scatter.23
  1061.5 27.6 reduce-scatter.25
  1098.9 27.2 reduce-scatter.17
  1128.3 25.7 reduce-scatter.15
  1156.5 25.7 reduce-scatter.19
  1186.0 69.9 reduce-scatter.29
  1259.4 71.2 reduce-scatter.31
  1338.6 27.8 all-gather.22
  1368.5 53.8 all-gather.18
  1423.8 27.9 all-gather.20
  1453.3 27.4 all-gather.24
  1482.2 27.4 all-gather.26
  1573.3 70.7 reduce-scatter.11
  1645.7 80.7 all-gather.32
  1728.6 68.2 all-gather.28
  1798.4 80.6 all-gather.30
  1880.7 79.2 all-gather.34
  2015.8 69.8 reduce-scatter.13
  2092.8 54.3 all-gather.36
  2149.5 76.7 reduce-scatter.27
  2228.7 77.2 reduce-scatter.21
  2308.1 77.2 reduce-scatter.23
  2387.6 27.6 reduce-scatter.25
  2424.9 27.2 reduce-scatter.17
  2454.3 25.7 reduce-scatter.15
  2482.5 25.7 reduce-scatter.19
  2512.2 69.9 reduce-scatter.29
  2585.6 71.2 reduce-scatter.31
